TPU v7x, 32 devices: a 4x4x1 block of a 4x4x8 slice. The times are simulated.
32 devices in a mesh: dp: 1 (over z), dcp: 32 (over y, x, core).
Axes of the slice: x: 4, y: 4, z: 1, core: 2. Of those that a mesh axis runs over, the one named last changes fastest.
The devices are a block of a 4x4x8 slice.
Arguments:
- q_abs: bfloat16 [128, 128, 576], P('dp', 'dcp')
- latent_cache: bfloat16 [128, 1, 32, 256, 576], P('dp', None, 'dcp')
- ctx_len: int32 [128], P('dp')
Outputs:
- output: bfloat16 [128, 128, 512], P(('dp', 'dcp'))
All inputs are finite; a program needn't handle non-finite values.
Results may differ from a plain program's by a relative error of at most 0.0061068.
Values are sent between devices in bfloat16 or wider.
A program may use at most 768 MiB of HBM per device.

v0:
```python
import functools
import math

import jax
import jax.numpy as jnp
from jax import lax
from jax.experimental import pallas as pl
from jax.experimental.pallas import tpu as pltpu
from jax.sharding import PartitionSpec as P

ROPE_DIM = 64
QK_DIM = 192
AXIS = 'dcp'
DEPTH = 3
SLICES = 4

FIRST, SECOND = 0, 1
FULL, LOW, HIGH = 0, 1, 2
GATHER = (
    (FIRST, 1, (0, 0), FULL, 0),
    (FIRST, -1, (0, 0), FULL, 1),
    (FIRST, 1, (-1, 0), LOW, 2),
    (FIRST, -1, (1, 0), HIGH, 2),
    (SECOND, 1, (0, 0), FULL, 3),
    (SECOND, 1, (-1, 0), FULL, 4),
    (SECOND, 1, (1, 0), FULL, 7),
    (SECOND, 1, (2, 0), FULL, 7),
    (SECOND, -1, (0, 0), FULL, 7),
    (SECOND, -1, (-1, 0), FULL, 7),
    (SECOND, -1, (1, 0), FULL, 5),
    (SECOND, -1, (2, 0), FULL, 6),
    (SECOND, 1, (0, -1), FULL, 7),
    (SECOND, 1, (-1, -1), FULL, 7),
    (SECOND, -1, (1, 1), FULL, 7),
    (SECOND, -1, (2, 1), FULL, 7),
)
REDUCE = ((2, LOW, 1, 0), (1, HIGH, 1, 2), (2, HIGH, -1, 1), (-1, LOW, -1, 2), (1, LOW, 1, 2), (-1, HIGH, -1, 2))


def _kernel(side, len_ref, q_ref, cache_ref, out_ref, sib_ref, q_sib, q_all, part, page, xbuf, ybuf, lse_x, lse_y,
            wgt, page_sem, swap_send, swap_recv, qs_send, qs_recv, ag_send, ag_recv, rs_send, rs_recv, last_recv, ls_send,
            ls_recv):
    nt, nj, own_heads, width = q_sib.shape
    heads, latent = part.shape[3:]
    page_len = page.shape[3]
    half_h, quarter_h = heads // 2, heads // 4
    tiles = q_all.shape[3]
    quarter_q, half_q = tiles // 4, tiles // 2
    columns = latent // 128

    me = lax.axis_index(AXIS)
    core = lax.rem(me, 2)
    xpos = lax.rem(me // 2, side)
    ypos = me // (2 * side)
    sibling = me + 1 - 2 * core

    def wrap(pos, step):
        return lax.rem(pos + (step + side), side)

    def neighbour(axis, half, step):
        if axis == half:
            return (ypos * side + wrap(xpos, step)) * 2 + core
        return (wrap(ypos, step) * side + xpos) * 2 + core

    def peer(dev):
        return {AXIS: dev}

    def remote(ref, dst, send_sem, recv_sem, dev):
        return pltpu.make_async_remote_copy(src_ref=ref, dst_ref=dst, send_sem=send_sem, recv_sem=recv_sem,
                                            device_id=peer(dev), device_id_type=pl.DeviceIdType.MESH)

    def gather_block(j, half, first, second, rng):
        if half == 0:
            yy, xx = wrap(ypos, second), wrap(xpos, first)
        else:
            yy, xx = wrap(ypos, first), wrap(xpos, second)
        start = half * half_q + (quarter_q if rng == HIGH else 0)
        return q_all.at[j, yy, xx, pl.ds(start, half_q if rng == FULL else quarter_q)]

    def gather_send(j, *indices):
        for idx in indices:
            for half in (0, 1):
                axis, step, (first, second), rng, sem = GATHER[idx]
                ref = gather_block(j, half, first, second, rng)
                remote(ref, ref, ag_send.at[j, 0 if rng == FULL else 1], ag_recv.at[j, sem],
                       neighbour(axis, half, step)).start()

    def wait_bytes(ref, sem):
        pltpu.make_async_copy(ref, ref, sem).wait()

    def gather_wait(j, sem):
        wait_bytes(q_all.at[j, pl.ds(0, side // 2)] if sem == 7 else q_all.at[j, 0, 0], ag_recv.at[j, sem])

    def rows_of(half, rng):
        return half * half_h + (quarter_h if rng == HIGH else 0)

    def first_part(r, half, step, rng, i=None):
        hs = pl.ds(rows_of(half, rng), quarter_h)
        second = slice(None) if i is None else i
        if half == 0:
            return part.at[r, second, wrap(xpos, step), hs]
        return part.at[r, wrap(ypos, step), second, hs]

    def second_part(r, half, step, rng):
        hs = pl.ds(rows_of(half, rng), quarter_h)
        if half == 0:
            return part.at[r, wrap(ypos, step), xpos, hs]
        return part.at[r, ypos, wrap(xpos, step), hs]

    def reduce_send(r, axis, *indices):
        for idx in indices:
            for half in (0, 1):
                dest, rng, step, sem = REDUCE[idx]
                src = (first_part if axis == FIRST else second_part)(r, half, dest, rng)
                dst = (xbuf if axis == FIRST else ybuf).at[r, half, idx]
                remote(src, dst, rs_send.at[r, axis], rs_recv.at[r, axis, sem], neighbour(axis, half, step)).start()

    def reduce_wait(r, axis, sem):
        buf = xbuf if axis == FIRST else ybuf
        wait_bytes(buf.at[r, :, pl.ds(0, 4)] if sem == 2 else buf.at[r, 0, pl.ds(0, 2)], rs_recv.at[r, axis, sem])

    def lse_buf(axis):
        return lse_x if axis == 0 else lse_y

    def lse_send(j, axis):
        buf = lse_buf(axis)
        for idx, step in enumerate((1, -1, 2)):
            remote(buf.at[j, 0], buf.at[j, idx + 1], ls_send.at[j, axis], ls_recv.at[j, axis], neighbour(axis, 0, step)).start()

    def lse_wait(j, axis):
        wait_bytes(lse_buf(axis).at[j, pl.ds(0, 3)], ls_recv.at[j, axis])

    def swap_piece(j, n):
        ts = pl.ds(n * (nt // SLICES), nt // SLICES)
        remote(cache_ref.at[ts, 1 - core, j], sib_ref.at[j, ts], swap_send.at[j], swap_recv.at[j], sibling).start()

    def query_swap():
        return remote(q_ref.at[:, 1 - core], q_sib, qs_send, qs_recv, sibling)

    def load_pages(n):
        slot, j, t = lax.rem(n, DEPTH), n // nt, lax.rem(n, nt)
        for p, src in ((0, cache_ref.at[t, core, j]), (1, sib_ref.at[j, t])):
            pltpu.make_async_copy(src, page.at[slot, p, pl.ds(0, width)], page_sem.at[slot, p]).start()
            pltpu.make_async_copy(src.at[pl.ds(latent, ROPE_DIM)], page.at[slot, p, pl.ds(width, ROPE_DIM)],
                                  page_sem.at[slot, p]).start()

    def merge_queries(j):
        for t in range(nt):
            mine = q_ref[t, core, j].astype(jnp.float32)
            other = q_sib[t, j].astype(jnp.float32)
            both = jnp.concatenate([jnp.where(core == 0, mine, other), jnp.where(core == 0, other, mine)], axis=0)
            base, sub = (t // 4) * quarter_q, t % 4
            for i in range(columns):
                q_all[j, ypos, xpos, base + sub * columns + i] = both[:, i * 128:(i + 1) * 128].astype(jnp.bfloat16)
            rope = both[:, latent:]
            if sub < 2:
                low = (low if sub else []) + [rope]
            else:
                q_all[j, ypos, xpos, base + 4 * columns + sub - 2] = jnp.concatenate([low[sub - 2], rope], axis=1).astype(
                    jnp.bfloat16)

    def gather_first(j):
        for sem, sends in ((0, (2, 5, 9)), (1, (3, 6, 10))):
            gather_wait(j, sem)
            gather_send(j, *sends)

    def gather_turn(j):
        gather_wait(j, 2)
        gather_send(j, 7, 11)

    def gather_second(j, sem, send):
        gather_wait(j, sem)
        gather_send(j, send)

    def gather_end(j):
        gather_wait(j, 7)

    def swap_wait(j):
        wait_bytes(sib_ref.at[j], swap_recv.at[j])

    def attend(n):
        @pl.when(n + DEPTH - 1 < nj * nt)
        def _():
            load_pages(n + DEPTH - 1)

        slot, j, t = lax.rem(n, DEPTH), n // nt, lax.rem(n, nt)
        for p in (0, 1):
            wait_bytes(page.at[slot, p], page_sem.at[slot, p])
        base, sub = (t // 4) * quarter_q, lax.rem(t, 4)
        cols = [q_all[j, :, :, base + sub * columns + i].reshape(heads, 128) for i in range(columns)]
        rope = q_all[j, :, :, base + 4 * columns + lax.rem(sub, 2)].reshape(heads, 128)
        lane_half = lax.broadcasted_iota(jnp.int32, (heads, 128), 1) // ROPE_DIM
        cols.append(jnp.where(lane_half == sub // 2, rope, jnp.zeros_like(rope)))
        q = jnp.concatenate(cols, axis=1)
        limit = len_ref[(t * 2 + core) * nj + j]
        outs, lses = [], []
        for p in (0, 1):
            owner = me if p == 0 else sibling
            s = jnp.dot(q, page[slot, p], preferred_element_type=jnp.float32) * (QK_DIM ** -0.5)
            position = owner * page_len + lax.broadcasted_iota(jnp.int32, (1, page_len), 1)
            s = jnp.where(position < limit, s, -1e30)
            m = jnp.max(s, axis=1, keepdims=True)
            w = jnp.exp(s - m)
            l = jnp.sum(w, axis=1, keepdims=True)
            pv = lax.dot_general(w.astype(jnp.bfloat16), page[slot, p, :latent], (((1,), (1,)), ((), ())),
                                 preferred_element_type=jnp.float32)
            outs.append((pv * (1.0 / l)).astype(jnp.bfloat16).astype(jnp.float32))
            lses.append(m + jnp.log(l))
        top = jnp.maximum(lses[0], lses[1])
        both = top + jnp.log(jnp.exp(lses[0] - top) + jnp.exp(lses[1] - top))
        part[j, t // side, lax.rem(t, side)] = jnp.exp(lses[0] - both) * outs[0] + jnp.exp(lses[1] - both) * outs[1]
        row = jnp.broadcast_to(both, (heads, 128)).T
        lse_x[j, 0, pl.ds(t, 1), :] = row[0:1]

    def combine(v):
        top = jnp.max(v, axis=0)
        return top + jnp.log(jnp.sum(jnp.exp(v - top[None]), axis=0))

    def lse_turn(j):
        lse_wait(j, 0)
        lse_y[j, 0] = combine(lse_x[j])
        lse_send(j, 1)

    def weigh(j):
        lse_wait(j, 1)
        wgt[...] = jnp.exp(lse_x[j, 0] - combine(lse_y[j]))

        def body(t, _):
            w = jnp.broadcast_to(wgt[pl.ds(t, 1), :], (128, heads)).T
            yy, xx = t // side, lax.rem(t, side)
            for i in range(latent // 128):
                cols = pl.ds(i * 128, 128)
                part[j, yy, xx, :, cols] = part[j, yy, xx, :, cols] * w
            return 0

        lax.fori_loop(0, nt, body, 0)

    def reduce_turn(r, axis):
        for idx, dest, rng, nxt, sem in ((0, 1, LOW, 4, 0), (2, -1, HIGH, 5, 1)):
            reduce_wait(r, axis, sem)
            for half in (0, 1):
                if axis == FIRST:
                    def body(i, _):
                        ref = first_part(r, half, dest, rng, i)
                        ref[...] = ref[...] + xbuf[r, half, idx, i]
                        return 0
                    lax.fori_loop(0, side, body, 0)
                else:
                    ref = second_part(r, half, dest, rng)
                    ref[...] = ref[...] + ybuf[r, half, idx]
            reduce_send(r, axis, nxt)

    def reduce_end(r, axis):
        reduce_wait(r, axis, 2)
        for half in (0, 1):
            for rng, one, two in ((HIGH, 1, 5), (LOW, 3, 4)):
                if axis == FIRST:
                    def body(i, _):
                        ref = first_part(r, half, 0, rng, i)
                        ref[...] = ref[...] + (xbuf[r, half, one, i] + xbuf[r, half, two, i])
                        return 0
                    lax.fori_loop(0, side, body, 0)
                else:
                    total = second_part(r, half, 0, rng)[...] + (ybuf[r, half, one] + ybuf[r, half, two])
                    out_ref[r, pl.ds(rows_of(half, rng), quarter_h)] = total.astype(out_ref.dtype)

    PIECES = ((2,), (1, -1), (0,))

    def row_of(half, step):
        return wrap(ypos if half == 0 else xpos, step)

    def last_turn(r):
        for sem in (0, 1):
            reduce_wait(r, FIRST, sem)
        for n, piece in enumerate(PIECES):
            for step in piece:
                for lane, (idx, dest, rng, nxt) in enumerate(((0, 1, LOW, 4), (2, -1, HIGH, 5))):
                    for half in (0, 1):
                        i = row_of(half, step)
                        ref = first_part(r, half, dest, rng, i)
                        ref[...] = ref[...] + xbuf[r, half, idx, i]
                        remote(ref, xbuf.at[r, half, nxt, i], rs_send.at[r, FIRST], last_recv.at[lane, n],
                               neighbour(FIRST, half, REDUCE[nxt][2])).start()

    def last_piece(r, n):
        if n == 0:
            wait_bytes(xbuf.at[r, 0, pl.ds(0, 4)], rs_recv.at[r, FIRST, 2])
        for lane in (0, 1):
            wait_bytes(xbuf.at[r, 0, 0, pl.ds(0, 2 * len(PIECES[n]))], last_recv.at[lane, n])
        for half in (0, 1):
            for step in PIECES[n]:
                i = row_of(half, step)
                for rng, one, two in ((HIGH, 1, 5), (LOW, 3, 4)):
                    ref = first_part(r, half, 0, rng, i)
                    ref[...] = ref[...] + (xbuf[r, half, one, i] + xbuf[r, half, two, i])
        if n < 2:
            reduce_send(r, SECOND, *((0, 2), (1, 3))[n])

    barrier = pltpu.get_barrier_semaphore()
    peers = [sibling] + [neighbour(axis, 0, step) for axis in (0, 1) for step in (1, -1, 2)]
    for dev in peers:
        pl.semaphore_signal(barrier, inc=1, device_id=peer(dev), device_id_type=pl.DeviceIdType.MESH)
    with jax.named_scope('barrier'):
        pl.semaphore_wait(barrier, len(peers))

    query_swap().start()
    with jax.named_scope('merge0'):
        query_swap().wait_recv()
        merge_queries(0)
    gather_send(0, 0, 1, 4, 8)
    swap_piece(0, 0)
    swap_piece(0, 1)
    with jax.named_scope('merges'):
        lax.fori_loop(1, nj, lambda j, _: (merge_queries(j), 0)[1], 0)
    with jax.named_scope('chunk0'):
        gather_first(0)
        swap_piece(0, 2)
        gather_second(0, 3, 12)
        gather_turn(0)
        gather_send(1, 0, 1)
        swap_piece(0, 3)
        gather_second(0, 4, 13)
        gather_second(0, 5, 14)
        gather_second(0, 6, 15)
    with jax.named_scope('chunk1'):
        swap_piece(1, 0)
        gather_first(1)
        gather_send(1, 4, 8)
        gather_send(2, 0, 1)
        swap_piece(1, 1)
        swap_wait(0)
        for n in range(DEPTH - 1):
            load_pages(n)
        gather_end(0)

    def run(*steps):
        for fn, *args in steps:
            with jax.named_scope(fn.__name__ + '_' + '_'.join(str(a) for a in args)):
                fn(*args)

    def middle(j):
        run((gather_turn, j), (gather_second, j, 4, 13), (gather_second, j, 5, 14), (gather_second, j, 3, 12))

    slots = {
        0: ((swap_piece, 1, 2),),
        1: ((gather_send, 2, 4, 8), (gather_send, 3, 0, 1), (swap_piece, 1, 3)),
        2: ((gather_turn, 1), (gather_second, 1, 4, 13), (gather_second, 1, 5, 14), (swap_piece, 2, 0)),
        3: ((gather_second, 1, 3, 12), (gather_first, 2), (swap_wait, 1), (swap_piece, 2, 1)),
        4: ((lse_send, 0, 0), (gather_second, 1, 6, 15), (gather_second, 2, 3, 12), (gather_send, 3, 4, 8), (lse_turn, 0),
            (gather_turn, 2), (gather_end, 1), (gather_second, 2, 4, 13), (gather_second, 2, 5, 14), (gather_first, 3),
            (swap_piece, 2, 2)),
        5: ((gather_second, 2, 6, 15), (swap_piece, 2, 3)),
        6: ((gather_turn, 3), (gather_second, 3, 3, 12), (weigh, 0), (reduce_send, 0, FIRST, 0, 2), (swap_piece, 3, 0)),
        7: ((gather_second, 3, 4, 13), (gather_second, 3, 5, 14), (swap_wait, 2), (swap_piece, 3, 1)),
        8: ((lse_send, 1, 0), (gather_second, 3, 6, 15), (gather_end, 2), (swap_piece, 3, 2)),
        9: ((reduce_send, 0, FIRST, 1, 3), (swap_piece, 3, 3)),
        11: ((lse_turn, 1), (reduce_turn, 0, FIRST), (swap_wait, 3)),
        12: ((lse_send, 2, 0), (gather_end, 3)),
        13: ((weigh, 1), (reduce_send, 1, FIRST, 0, 2)),
        14: ((lse_turn, 2),),
        15: ((reduce_send, 1, FIRST, 1, 3),),
    }

    def slot_body(n, _):
        for at, steps in slots.items():
            pl.when(n == at)(functools.partial(run, *steps))
        with jax.named_scope('attend'):
            lax.fori_loop(n * (nt // SLICES), (n + 1) * (nt // SLICES), lambda i, _: (attend(i), 0)[1], 0)
        return 0

    lax.fori_loop(0, nj * SLICES, slot_body, 0)

    early = (0, 2, 1, 3)
    run((lse_send, 3, 0), (reduce_end, 0, FIRST), (reduce_send, 0, SECOND, *early))
    run((reduce_turn, 1, FIRST), (reduce_turn, 0, SECOND), (lse_turn, 3), (weigh, 2), (reduce_send, 2, FIRST, *early),
        (reduce_end, 1, FIRST), (reduce_send, 1, SECOND, *early), (reduce_end, 0, SECOND))
    run((reduce_turn, 2, FIRST), (reduce_turn, 1, SECOND), (weigh, 3), (reduce_send, 3, FIRST, *early),
        (reduce_end, 2, FIRST), (reduce_send, 2, SECOND, *early), (reduce_end, 1, SECOND))
    run((last_turn, 3), (last_piece, 3, 0), (reduce_turn, 2, SECOND), (last_piece, 3, 1), (last_piece, 3, 2))
    run((reduce_turn, 3, SECOND), (reduce_end, 2, SECOND), (reduce_end, 3, SECOND))

    def drain(j, _):
        wait_bytes(sib_ref.at[j], swap_send.at[j])
        wait_bytes(q_all.at[j, :, :, pl.ds(0, 14 * tiles // 16)], ag_send.at[j, 0])
        wait_bytes(q_all.at[j, 0, 0], ag_send.at[j, 1])
        wait_bytes(xbuf.at[j], rs_send.at[j, 0])
        wait_bytes(ybuf.at[j], rs_send.at[j, 1])
        for axis in (0, 1):
            wait_bytes(lse_buf(axis).at[j, pl.ds(0, 3)], ls_send.at[j, axis])
        return 0

    with jax.named_scope('drain'):
        query_swap().wait_send()
        lax.fori_loop(0, nj, drain, 0)


def solution(mesh):
    group_size = mesh.shape[AXIS]
    side = math.isqrt(group_size // 2)
    nt = side * side

    def local_step(q_blk, cache_blk, len_blk):
        batch_rows, own_heads, width = q_blk.shape
        page_len = cache_blk.shape[3]
        latent = width - ROPE_DIM
        nj = batch_rows // group_size
        heads = 2 * own_heads * nt
        tiles = nt * (latent // 128) + nt // 2
        q = q_blk.reshape(nt, 2, nj, own_heads, width)
        cache = jnp.swapaxes(cache_blk.reshape(nt, 2, nj, page_len, width), 3, 4)
        any_space = pl.BlockSpec(memory_space=pl.ANY)
        dma = pltpu.SemaphoreType.DMA
        out, _ = pl.pallas_call(
            functools.partial(_kernel, side),
            out_shape=(jax.ShapeDtypeStruct((nj, heads, latent), jnp.bfloat16),
                       jax.ShapeDtypeStruct((nj, nt, width, page_len), jnp.bfloat16)),
            in_specs=[pl.BlockSpec(memory_space=pltpu.SMEM), pl.BlockSpec(memory_space=pltpu.VMEM), any_space],
            out_specs=(pl.BlockSpec(memory_space=pltpu.VMEM), any_space),
            scratch_shapes=[
                pltpu.VMEM((nt, nj, own_heads, width), jnp.bfloat16),
                pltpu.VMEM((nj, side, side, tiles, 2 * own_heads, 128), jnp.bfloat16),
                pltpu.VMEM((nj, side, side, heads, latent), jnp.float32),
                pltpu.VMEM((DEPTH, 2, width + ROPE_DIM, page_len), jnp.bfloat16),
                pltpu.VMEM((nj, 2, len(REDUCE), side, heads // 4, latent), jnp.float32),
                pltpu.VMEM((nj, 2, len(REDUCE), heads // 4, latent), jnp.float32),
                pltpu.VMEM((nj, 4, nt, heads), jnp.float32),
                pltpu.VMEM((nj, 4, nt, heads), jnp.float32),
                pltpu.VMEM((nt, heads), jnp.float32),
                dma((DEPTH, 2)), dma((nj,)), dma((nj,)), dma(()), dma(()),
                dma((nj, 2)), dma((nj, 8)), dma((nj, 2)), dma((nj, 2, 3)), dma((2, 3)), dma((nj, 2)), dma((nj, 2)),
            ],
            compiler_params=pltpu.CompilerParams(collective_id=0, has_side_effects=True, vmem_limit_bytes=54_000_000),
        )(len_blk, q, cache)
        return out

    return jax.shard_map(local_step, mesh=mesh, in_specs=(P('dp', AXIS, None), P('dp', None, AXIS, None, None), P('dp')),
                         out_specs=P(('dp', AXIS), None, None), check_vma=False)
```

profile of v0, /device:TPU:96, one launch (start us, length us, event | category | flops | bytes accessed | tf_op | source)
XLA Modules:
  0.0 151.0 jit_solution(9543901075645541879)
XLA Ops:
  0.0 1.6 %copy.4 = bf16[128,4,576]{2,1,0:T(4,128)(2,1)S(1)} copy(bf16[128,4,576]{0,2,1:T(8,128)(2,1)} %param.3) | data formatting | bytes 1179648 | tf_op args[0]
  1.6 0.0 copy-start
  1.6 0.6 copy-done
  2.2 148.0 %shard_map.37 = (bf16[4,128,512]{2,1,0:T(8,128)(2,1)S(1)}, bf16[4,16,576,256]{3,2,1,0:T(8,128)(2,1)}) custom-call(s32[128]{0:T(128)S(1)} %copy-done, bf16[16,2,4,4,576]{4,3,2,1,0:T(4,128)(2,1)S(1)} %bitcast.4, bf16[16,2,4,576,256]{4,3,2,1,0:T(8,128)(2,1)} %bitcast.5), custom_call_target="tpu_custom_call" | custom-call | tf_op jit(solution)/shard_map/pallas_call | solution.py:413
  150.2 0.8 copy.6
Async XLA Ops:
  1.6 0.7 copy-start
where the time goes:
time: 151 us
  Pallas kernels  148 us (98%)
  local copies, waits for them, and re-layouts  3.02 us (2%)
    pallas_call x1, Pallas kernels, local_step(): pl.pallas_call(functools.partial(_kernel, side), out_shape=(jax.ShapeDtyp...  148 us
    unnamed x4, local copies, waits for them, and re-layouts  3.02 us

commit v1 on v0

--- a/solution.py
+++ b/solution.py
@@ -346,19 +346,17 @@
         1: ((gather_send, 2, 4, 8), (gather_send, 3, 0, 1), (swap_piece, 1, 3)),
         2: ((gather_turn, 1), (gather_second, 1, 4, 13), (gather_second, 1, 5, 14), (swap_piece, 2, 0)),
         3: ((gather_second, 1, 3, 12), (gather_first, 2), (swap_wait, 1), (swap_piece, 2, 1)),
-        4: ((lse_send, 0, 0), (gather_second, 1, 6, 15), (gather_second, 2, 3, 12), (gather_send, 3, 4, 8), (lse_turn, 0),
-            (gather_turn, 2), (gather_end, 1), (gather_second, 2, 4, 13), (gather_second, 2, 5, 14), (gather_first, 3),
-            (swap_piece, 2, 2)),
-        5: ((gather_second, 2, 6, 15), (swap_piece, 2, 3)),
-        6: ((gather_turn, 3), (gather_second, 3, 3, 12), (weigh, 0), (reduce_send, 0, FIRST, 0, 2), (swap_piece, 3, 0)),
-        7: ((gather_second, 3, 4, 13), (gather_second, 3, 5, 14), (swap_wait, 2), (swap_piece, 3, 1)),
-        8: ((lse_send, 1, 0), (gather_second, 3, 6, 15), (gather_end, 2), (swap_piece, 3, 2)),
+        4: ((lse_send, 0, 0), (gather_second, 1, 6, 15), (gather_second, 2, 3, 12), (gather_send, 3, 4, 8), (gather_turn, 2),
+            (gather_end, 1), (swap_piece, 2, 2)),
+        5: ((lse_turn, 0), (gather_second, 2, 4, 13), (gather_second, 2, 5, 14), (gather_first, 3), (swap_piece, 2, 3)),
+        6: ((gather_second, 2, 6, 15), (gather_second, 3, 3, 12), (weigh, 0), (reduce_send, 0, FIRST, 0, 2), (swap_piece, 3, 0)),
+        7: ((gather_turn, 3), (gather_second, 3, 4, 13), (gather_second, 3, 5, 14), (swap_wait, 2), (swap_piece, 3, 1)),
+        8: ((lse_send, 1, 0), (gather_end, 2), (swap_piece, 3, 2)),
         9: ((reduce_send, 0, FIRST, 1, 3), (swap_piece, 3, 3)),
+        10: ((gather_second, 3, 6, 15),),
         11: ((lse_turn, 1), (reduce_turn, 0, FIRST), (swap_wait, 3)),
-        12: ((lse_send, 2, 0), (gather_end, 3)),
-        13: ((weigh, 1), (reduce_send, 1, FIRST, 0, 2)),
-        14: ((lse_turn, 2),),
-        15: ((reduce_send, 1, FIRST, 1, 3),),
+        12: ((lse_send, 2, 0), (gather_end, 3), (weigh, 1), (reduce_send, 1, FIRST, 0, 2)),
+        14: ((lse_turn, 2), (reduce_send, 1, FIRST, 1, 3)),
     }
 
     def slot_body(n, _):

time: 151 us -> 151 us (level)
  no operation moved by 1% of the time
where the time goes in v1:
time: 151 us
  Pallas kernels  148 us (98%)
  local copies, waits for them, and re-layouts  3.02 us (2%)
    pallas_call x1, Pallas kernels, local_step(): pl.pallas_call(functools.partial(_kernel, side), out_shape=(jax.ShapeDtyp...  148 us
    unnamed x4, local copies, waits for them, and re-layouts  3.02 us

profile of v1, /device:TPU:96, one launch (start us, length us, event | category | flops | bytes accessed | tf_op | source)
XLA Modules:
  0.0 151.1 jit_solution(9705559266620232)
XLA Ops:
  0.0 1.6 %copy.4 = bf16[128,4,576]{2,1,0:T(4,128)(2,1)S(1)} copy(bf16[128,4,576]{0,2,1:T(8,128)(2,1)} %param.3) | data formatting | bytes 1179648 | tf_op args[0]
  1.6 0.0 copy-start
  1.6 0.6 copy-done
  2.2 148.0 %shard_map.37 = (bf16[4,128,512]{2,1,0:T(8,128)(2,1)S(1)}, bf16[4,16,576,256]{3,2,1,0:T(8,128)(2,1)}) custom-call(s32[128]{0:T(128)S(1)} %copy-done, bf16[16,2,4,4,576]{4,3,2,1,0:T(4,128)(2,1)S(1)} %bitcast.4, bf16[16,2,4,576,256]{4,3,2,1,0:T(8,128)(2,1)} %bitcast.5), custom_call_target="tpu_custom_call" | custom-call | tf_op jit(solution)/shard_map/pallas_call | solution.py:411
  150.3 0.8 copy.6
Async XLA Ops:
  1.6 0.7 copy-start

commit v2 on v0

--- a/solution.py
+++ b/solution.py
@@ -82,7 +82,7 @@
             for half in (0, 1):
                 axis, step, (first, second), rng, sem = GATHER[idx]
                 ref = gather_block(j, half, first, second, rng)
-                remote(ref, ref, ag_send.at[j, 0 if rng == FULL else 1], ag_recv.at[j, sem],
+                remote(ref, ref, ag_send.at[0 if rng == FULL else 1], ag_recv.at[j, sem],
                        neighbour(axis, half, step)).start()
 
     def wait_bytes(ref, sem):
@@ -113,7 +113,7 @@
                 dest, rng, step, sem = REDUCE[idx]
                 src = (first_part if axis == FIRST else second_part)(r, half, dest, rng)
                 dst = (xbuf if axis == FIRST else ybuf).at[r, half, idx]
-                remote(src, dst, rs_send.at[r, axis], rs_recv.at[r, axis, sem], neighbour(axis, half, step)).start()
+                remote(src, dst, rs_send.at[axis], rs_recv.at[r, axis, sem], neighbour(axis, half, step)).start()
 
     def reduce_wait(r, axis, sem):
         buf = xbuf if axis == FIRST else ybuf
@@ -125,14 +125,14 @@
     def lse_send(j, axis):
         buf = lse_buf(axis)
         for idx, step in enumerate((1, -1, 2)):
-            remote(buf.at[j, 0], buf.at[j, idx + 1], ls_send.at[j, axis], ls_recv.at[j, axis], neighbour(axis, 0, step)).start()
+            remote(buf.at[j, 0], buf.at[j, idx + 1], ls_send.at[axis], ls_recv.at[j, axis], neighbour(axis, 0, step)).start()
 
     def lse_wait(j, axis):
         wait_bytes(lse_buf(axis).at[j, pl.ds(0, 3)], ls_recv.at[j, axis])
 
     def swap_piece(j, n):
         ts = pl.ds(n * (nt // SLICES), nt // SLICES)
-        remote(cache_ref.at[ts, 1 - core, j], sib_ref.at[j, ts], swap_send.at[j], swap_recv.at[j], sibling).start()
+        remote(cache_ref.at[ts, 1 - core, j], sib_ref.at[j, ts], swap_send, swap_recv.at[j], sibling).start()
 
     def query_swap():
         return remote(q_ref.at[:, 1 - core], q_sib, qs_send, qs_recv, sibling)
@@ -279,7 +279,7 @@
                         i = row_of(half, step)
                         ref = first_part(r, half, dest, rng, i)
                         ref[...] = ref[...] + xbuf[r, half, idx, i]
-                        remote(ref, xbuf.at[r, half, nxt, i], rs_send.at[r, FIRST], last_recv.at[lane, n],
+                        remote(ref, xbuf.at[r, half, nxt, i], rs_send.at[FIRST], last_recv.at[lane, n],
                                neighbour(FIRST, half, REDUCE[nxt][2])).start()
 
     def last_piece(r, n):
@@ -379,19 +379,14 @@
     run((last_turn, 3), (last_piece, 3, 0), (reduce_turn, 2, SECOND), (last_piece, 3, 1), (last_piece, 3, 2))
     run((reduce_turn, 3, SECOND), (reduce_end, 2, SECOND), (reduce_end, 3, SECOND))
 
-    def drain(j, _):
-        wait_bytes(sib_ref.at[j], swap_send.at[j])
-        wait_bytes(q_all.at[j, :, :, pl.ds(0, 14 * tiles // 16)], ag_send.at[j, 0])
-        wait_bytes(q_all.at[j, 0, 0], ag_send.at[j, 1])
-        wait_bytes(xbuf.at[j], rs_send.at[j, 0])
-        wait_bytes(ybuf.at[j], rs_send.at[j, 1])
-        for axis in (0, 1):
-            wait_bytes(lse_buf(axis).at[j, pl.ds(0, 3)], ls_send.at[j, axis])
-        return 0
-
-    with jax.named_scope('drain'):
-        query_swap().wait_send()
-        lax.fori_loop(0, nj, drain, 0)
+    query_swap().wait_send()
+    wait_bytes(sib_ref, swap_send)
+    wait_bytes(q_all.at[:, :, :, pl.ds(0, 14 * tiles // 16)], ag_send.at[0])
+    wait_bytes(q_all.at[:, 0, 0], ag_send.at[1])
+    wait_bytes(xbuf, rs_send.at[0])
+    wait_bytes(ybuf, rs_send.at[1])
+    for axis in (0, 1):
+        wait_bytes(lse_buf(axis).at[:, pl.ds(0, 3)], ls_send.at[axis])
 
 
 def solution(mesh):
@@ -426,8 +421,8 @@
                 pltpu.VMEM((nj, 4, nt, heads), jnp.float32),
                 pltpu.VMEM((nj, 4, nt, heads), jnp.float32),
                 pltpu.VMEM((nt, heads), jnp.float32),
-                dma((DEPTH, 2)), dma((nj,)), dma((nj,)), dma(()), dma(()),
-                dma((nj, 2)), dma((nj, 8)), dma((nj, 2)), dma((nj, 2, 3)), dma((2, 3)), dma((nj, 2)), dma((nj, 2)),
+                dma((DEPTH, 2)), dma(()), dma((nj,)), dma(()), dma(()),
+                dma((2,)), dma((nj, 8)), dma((2,)), dma((nj, 2, 3)), dma((2, 3)), dma((2,)), dma((nj, 2)),
             ],
             compiler_params=pltpu.CompilerParams(collective_id=0, has_side_effects=True, vmem_limit_bytes=54_000_000),
         )(len_blk, q, cache)

time: 151 us -> 151 us (level)
  no operation moved by 1% of the time
where the time goes in v2:
time: 151 us
  Pallas kernels  148 us (98%)
  local copies, waits for them, and re-layouts  3.02 us (2%)
    pallas_call x1, Pallas kernels, local_step(): pl.pallas_call(functools.partial(_kernel, side), out_shape=(jax.ShapeDtyp...  148 us
    unnamed x4, local copies, waits for them, and re-layouts  3.02 us

profile of v2, /device:TPU:96, one launch (start us, length us, event | category | flops | bytes accessed | tf_op | source)
XLA Modules:
  0.0 150.8 jit_solution(14444780342447215166)
XLA Ops:
  0.0 1.6 %copy.4 = bf16[128,4,576]{2,1,0:T(4,128)(2,1)S(1)} copy(bf16[128,4,576]{0,2,1:T(8,128)(2,1)} %param.3) | data formatting | bytes 1179648 | tf_op args[0]
  1.6 0.0 copy-start
  1.6 0.6 copy-done
  2.2 147.8 %shard_map.37 = (bf16[4,128,512]{2,1,0:T(8,128)(2,1)S(1)}, bf16[4,16,576,256]{3,2,1,0:T(8,128)(2,1)}) custom-call(s32[128]{0:T(128)S(1)} %copy-done, bf16[16,2,4,4,576]{4,3,2,1,0:T(4,128)(2,1)S(1)} %bitcast.4, bf16[16,2,4,576,256]{4,3,2,1,0:T(8,128)(2,1)} %bitcast.5), custom_call_target="tpu_custom_call" | custom-call | tf_op jit(solution)/shard_map/pallas_call | solution.py:408
  150.0 0.8 copy.6
Async XLA Ops:
  1.6 0.7 copy-start
